TPU v7x, 32 devices: a whole 2x2x4 slice. The times are simulated.
32 devices in a mesh: row: 8 (over z, x), col: 4 (over y, core).
Axes of the slice: x: 2, y: 2, z: 4, core: 2. Of those that a mesh axis runs over, the one named last changes fastest.
Arguments:
- tiles: bfloat16 [8, 4, 3, 256, 256], P('row', 'col'), as said below
- stack_index: int32 [8, 4, 3], P('row', 'col'), may hold values from 0 to 127, as said below
- block_mask: int32 [64, 64], replicated, may hold values from 0 to 1, as said below
Outputs:
- purified: bfloat16 [8, 4, 3, 256, 256], P('row', 'col')
Inputs may be any that keep to these rules, and one draw needn't show every extreme that they name: `block_mask`: the region of one device (8 x 16 blocks) holds at most 3 occupied blocks; some region holds exactly 3 in every draw. `stack_index`: block (a, b) of a device's region is numbered a * 16 + b. A device's 3 entries are distinct and include every occupied block of its region; a slot naming an unoccupied block holds a tile that P does not use. `tiles`: A slot's tile is P's block named by stack_index when that block is occupied.
All inputs are finite; a program needn't handle non-finite values.
Results may differ from a plain program's by a relative error of at most 0.0051.
Values may be sent and summed in bfloat16 or wider, within the bound.
A program may use at most 64 MiB of HBM per device.

v0:
```python
import functools

import jax
import jax.numpy as jnp
from jax import lax
from jax.experimental import pallas as pl
from jax.experimental.pallas import tpu as pltpu
from jax.sharding import PartitionSpec as P

MESH = pl.DeviceIdType.MESH
VMEM = pl.BlockSpec(memory_space=pltpu.VMEM)
SMEM = pl.BlockSpec(memory_space=pltpu.SMEM)


def send(src, dst, send_sem, recv_sem, row, col):
    return pltpu.make_async_remote_copy(
        src_ref=src,
        dst_ref=dst,
        send_sem=send_sem,
        recv_sem=recv_sem,
        device_id=(row, col),
        device_id_type=MESH,
    )


def greet(row_size, col_size, row, col, with_rows):
    barrier = pltpu.get_barrier_semaphore()
    count = col_size - 1
    for step in range(1, col_size):
        peer = lax.rem(col + step, col_size)
        pl.semaphore_signal(barrier, inc=1, device_id=(row, peer), device_id_type=MESH)
    if with_rows:
        count += row_size - 1
        for step in range(1, row_size):
            peer = lax.rem(row + step, row_size)
            pl.semaphore_signal(barrier, inc=1, device_id=(peer, col), device_id_type=MESH)
    pl.semaphore_wait(barrier, count)


class ColGather:
    def __init__(self, row, col, col_size, slots, own, panel, sems):
        self.row, self.col, self.slots = row, col, slots
        self.own, self.panel, self.sems = own, panel, sems
        self.chips = col_size // 2
        self.chip, self.core = col // 2, lax.rem(col, 2)
        self.partner = col + 1 - 2 * self.core

    def across(self, step, slot):
        target = 2 * lax.rem(self.chip + step, self.chips) + self.core
        return send(
            self.own.at[slot], self.panel.at[self.col, slot],
            self.sems.at[0, step - 1, slot], self.sems.at[1, step - 1, slot], self.row, target,
        )

    def beside(self, step, slot):
        origin = 2 * lax.rem(self.chip + self.chips - step, self.chips) + self.core
        src = self.own.at[slot] if step == 0 else self.panel.at[origin, slot]
        return send(
            src, self.panel.at[origin, slot],
            self.sems.at[2, step, slot], self.sems.at[3, step, slot], self.row, self.partner,
        )

    def start(self):
        for slot in range(self.slots):
            for step in range(1, self.chips):
                self.across(step, slot).start()
        for slot in range(self.slots):
            self.beside(0, slot).start()

    def origin(self, step, core):
        return 2 * lax.rem(self.chip + self.chips - step, self.chips) + core

    def forward(self, use=None):
        for slot in range(self.slots):
            for step in range(1, self.chips):
                self.across(step, slot).wait_recv()
                self.beside(step, slot).start()
                if use is not None:
                    use(self.origin(step, self.core), slot)

    def collect(self, use, steps):
        for step in steps:
            for slot in range(self.slots):
                self.beside(step, slot).wait_recv()
                if use is not None:
                    use(self.origin(step, 1 - self.core), slot)

    def settle(self):
        for step in range(self.chips):
            for slot in range(self.slots):
                if step:
                    self.across(step, slot).wait_send()
                self.beside(step, slot).wait_send()


def kernel(
    row_size, col_size, tiles, ids, mask, out, left, right, squares, square, total, left_ids, right_ids, ids_out,
    left_labels, right_labels, col_sems, square_sems, line_sems, side_sems, row_id_sems, col_id_sems, label_sems,
):
    row, col = lax.axis_index("row"), lax.axis_index("col")
    slots, side = tiles.shape[0], tiles.shape[1]
    half = side // 2
    length = row_size // 2
    place, lane = row // 2, lax.rem(row, 2)
    mate = row + 1 - 2 * lane

    lane_iota = lax.broadcasted_iota(jnp.int32, (8, 128), 1)
    packed = jnp.full((8, 128), -1, jnp.int32)
    for slot in range(slots):
        packed = jnp.where(lane_iota == slot, ids[0, slot], packed)
    ids_out[...] = packed
    greet(row_size, col_size, row, col, True)

    pieces = [(slot, 0, side, False) for slot in range(slots - 1)]
    cut = side * 64 // 256
    pieces += [(slots - 1, cut, side - cut, False)]
    early = (slots - 1, 0, cut, True)
    mine = [early] + pieces
    count = len(mine)

    def view(ref, piece, origin=None):
        slot, first, rows, _ = piece
        if origin is None:
            return ref.at[slot, pl.ds(first, rows)]
        return ref.at[origin, slot, pl.ds(first, rows)]

    def to_mate(index, at):
        piece = mine[index]
        origin = 2 * at + lane
        return send(
            view(right, piece, origin), view(right, piece, origin),
            side_sems.at[0, at, index], side_sems.at[1, at, index], mate, col,
        )

    def own_to_mate(index):
        piece = mine[index]
        return send(
            view(tiles, piece), view(right, piece, row),
            side_sems.at[0, place, index], side_sems.at[1, place, index], mate, col,
        )

    def from_mate(index, at):
        piece = mine[index]
        origin = 2 * at + 1 - lane
        return send(
            view(right, piece, origin), view(right, piece, origin),
            side_sems.at[0, at, index], side_sems.at[1, at, index], mate, col,
        )

    def along(way, step, index, first=False):
        heading = 1 if way == 0 else -1
        piece = mine[0] if index == count else mine[index]
        on_lane = 1 - lane if index == count else lane
        origin = 2 * (place - heading * step) + on_lane
        src = view(tiles, piece) if first and index < count else view(right, piece, origin)
        return send(
            src, view(right, piece, origin),
            line_sems.at[way, 0, step, index], line_sems.at[way, 1, step, index],
            row + 2 * heading, col,
        )

    def landing(way, step, index):
        heading = 1 if way == 0 else -1
        piece = mine[0] if index == count else mine[index]
        on_lane = 1 - lane if index == count else lane
        origin = 2 * (place - heading * (step + 1)) + on_lane
        return send(
            view(right, piece, origin), view(right, piece, origin),
            line_sems.at[way, 0, step, index], line_sems.at[way, 1, step, index],
            row + 2 * heading, col,
        )

    can_send = (place + 1 < length, place > 0)

    def arrives(way, step):
        return place - step >= 1 if way == 0 else place + step + 1 < length

    def goes(way, step):
        if way == 0:
            return (place - step >= 0) & (place + 1 < length)
        return (place + step < length) & (place > 0)

    def id_row(step):
        return send(
            ids_out, right_ids.at[row], row_id_sems.at[0, step], row_id_sems.at[1, step],
            lax.rem(row + step, row_size), col,
        )

    def id_col(step):
        return send(
            ids_out, left_ids.at[col], col_id_sems.at[0, step], col_id_sems.at[1, step],
            row, lax.rem(col + step, col_size),
        )

    for step in range(1, row_size):
        id_row(step).start()
    for step in range(1, col_size):
        id_col(step).start()

    left_gather = ColGather(row, col, col_size, slots, tiles, left, col_sems)
    left_gather.start()
    own_to_mate(0).start()
    for index in range(count):
        for way in range(2):
            @pl.when(can_send[way])
            def _():
                along(way, 0, index, True).start()
        if index:
            own_to_mate(index).start()


    from_mate(0, place).wait_recv()
    for way in range(2):
        @pl.when(can_send[way])
        def _():
            along(way, 0, count).start()

    right[row] = tiles[...]
    left[col] = tiles[...]
    right_ids[row] = packed
    left_ids[col] = packed

    def turn(step, unused):
        for index in list(range(count)) + [count]:
            for way in range(2):
                @pl.when(arrives(way, step))
                def _():
                    landing(way, step, index).wait_recv()

                    @pl.when(can_send[way])
                    def _():
                        along(way, step + 1, index).start()

                    if 0 < index < count:
                        heading = 1 if way == 0 else -1
                        to_mate(index, place - heading * (step + 1)).start()
        return unused

    block_rows, block_cols = mask.shape[0] // row_size, mask.shape[1] // col_size
    owns = []
    for slot in range(slots):
        own = ids[0, slot]
        own_row, own_col = own // block_cols, lax.rem(own, block_cols)
        out_row, out_col = row * block_rows + own_row, col * block_cols + own_col
        owns.append((own_row, own_col, out_row, out_col, mask[out_row, out_col] > 0))

    def find(labels, region, wanted):
        spot, found = jnp.int32(0), labels[region, 0, 0] == wanted
        for other in range(1, slots):
            same = labels[region, 0, other] == wanted
            spot = jnp.where(same, other, spot)
            found = found | same
        return spot, found

    def square_term(origin, place):
        label = right_labels[origin, 0, place]
        inner = origin * block_rows + label // block_cols
        band = inner // block_cols
        chosen = []
        for own_row, own_col, out_row, out_col, live in owns:
            spot, found = find(left_labels, band, own_row * block_cols + lax.rem(inner, block_cols))
            use = live & found & (lax.rem(label, block_cols) == own_col)
            use = use & (mask[out_row, inner] > 0) & (mask[inner, out_col] > 0)
            tile = left[band, spot]
            chosen.append(jnp.where(use, tile, jnp.zeros_like(tile)))
        term = jnp.dot(
            jnp.concatenate(chosen, axis=0), right[origin, place], preferred_element_type=jnp.float32
        )
        total[...] += term.reshape(total.shape)

    def cube_term(origin, place):
        label = left_labels[origin, 0, place]
        inner = origin * block_cols + lax.rem(label, block_cols)
        band = inner // block_rows
        piece = squares[origin, place]
        for slot, (own_row, own_col, out_row, out_col, live) in enumerate(owns):
            spot, found = find(right_labels, band, lax.rem(inner, block_rows) * block_cols + own_col)
            use = live & found & (label // block_cols == own_row)
            use = use & (mask[out_row, inner] > 0) & (mask[inner, out_col] > 0)
            tile = right[band, spot]
            total[slot] += jnp.dot(
                piece, jnp.where(use, tile, jnp.zeros_like(tile)), preferred_element_type=jnp.float32
            )

    def stack_terms(origin, wait=None):
        for slot in range(slots):
            if wait is not None:
                wait(slot)
            square_term(origin, slot)

    def mate_terms(at):
        stack_terms(2 * at + 1 - lane, lambda slot: from_mate(slot + 1, at).wait_recv())

    def consume(step):
        for way in range(2):
            @pl.when(arrives(way, step))
            def _():
                heading = 1 if way == 0 else -1
                stack_terms(2 * (place - heading * (step + 1)) + lane)
        for way in range(2):
            @pl.when(arrives(way, step))
            def _():
                heading = 1 if way == 0 else -1
                mate_terms(place - heading * (step + 1))

    total[...] = jnp.zeros_like(total)
    turn(0, 0)
    for step in range(1, row_size):
        id_row(step).wait()
    for step in range(1, col_size):
        id_col(step).wait()
    copies = (
        pltpu.make_async_copy(left_ids, left_labels, label_sems.at[0]),
        pltpu.make_async_copy(right_ids, right_labels, label_sems.at[1]),
    )
    for copy in copies:
        copy.start()
    for copy in copies:
        copy.wait()
    left_gather.forward()
    left_gather.collect(None, range(left_gather.chips))
    stack_terms(row)
    mate_terms(place)

    def advance(step, unused):
        turn(step, 0)
        consume(step - 1)
        return unused

    lax.fori_loop(1, length - 1, advance, 0)
    consume(length - 2)

    square[...] = total[...].astype(square.dtype)

    square_gather = ColGather(row, col, col_size, slots, square, squares, square_sems)

    def keep(slot, unused):
        squares[col, slot] = square[slot]
        for step in range(1, square_gather.chips):
            square_gather.across(step, slot).start()
        square_gather.beside(0, slot).start()
        return unused

    lax.fori_loop(0, slots, keep, 0)
    total[...] = jnp.zeros_like(total)
    for slot in range(slots):
        cube_term(col, slot)
    square_gather.collect(cube_term, [0])
    square_gather.forward(cube_term)
    square_gather.collect(cube_term, range(1, square_gather.chips))
    out[...] = (3.0 * square[...].astype(jnp.float32) - 2.0 * total[...]).astype(out.dtype)

    left_gather.settle()
    square_gather.settle()

    def settle(step, unused):
        for index in range(count + 1):
            for way in range(2):
                @pl.when(goes(way, step))
                def _():
                    along(way, step, index).wait_send()
        return unused

    lax.fori_loop(0, length - 1, settle, 0)
    own_to_mate(0).wait_send()

    def collect(at, unused):
        for index in range(1, count):
            to_mate(index, at).wait_send()
        return unused

    lax.fori_loop(0, length, collect, 0)


def solution(mesh):
    row_size, col_size = mesh.shape["row"], mesh.shape["col"]
    length, chips = row_size // 2, col_size // 2
    dma = pltpu.SemaphoreType.DMA

    def local(tiles, stack_index, block_mask):
        stack, ids = tiles[0, 0], stack_index[0]
        slots, side, _ = stack.shape
        col_panel = pltpu.VMEM((col_size, slots, side, side), stack.dtype)
        purified = pl.pallas_call(
            functools.partial(kernel, row_size, col_size),
            out_shape=jax.ShapeDtypeStruct(stack.shape, stack.dtype),
            in_specs=[VMEM, SMEM, SMEM],
            out_specs=VMEM,
            scratch_shapes=[
                col_panel,
                pltpu.VMEM((row_size, slots, side, side), stack.dtype),
                col_panel,
                pltpu.VMEM(stack.shape, stack.dtype),
                pltpu.VMEM(stack.shape, jnp.float32),
                pltpu.VMEM((col_size, 8, 128), jnp.int32),
                pltpu.VMEM((row_size, 8, 128), jnp.int32),
                pltpu.VMEM((8, 128), jnp.int32),
                pltpu.SMEM((col_size, 8, 128), jnp.int32),
                pltpu.SMEM((row_size, 8, 128), jnp.int32),
                dma((4, chips, slots)),
                dma((4, chips, slots)),
                dma((2, 2, length, slots + 2)),
                dma((2, length, slots + 1)),
                dma((2, row_size)),
                dma((2, col_size)),
                dma((2,)),
            ],
            compiler_params=pltpu.CompilerParams(collective_id=0, has_side_effects=True),
            name="purify",
        )(stack, ids, block_mask)
        return purified[None, None]

    placed = (P("row", "col", None, None, None), P("row", "col", None), P())
    return jax.shard_map(
        local,
        mesh=mesh,
        in_specs=placed,
        out_specs=P("row", "col", None, None, None),
        check_vma=False,
    )
```

profile of v0, /device:TPU:1, one launch (start us, length us, event | category | flops | bytes accessed | tf_op | source)
XLA Modules:
  0.0 56.0 jit_solution(4714833451662923179)
XLA Ops:
  0.0 54.3 %purify.1 = bf16[3,256,256]{2,1,0:T(8,128)(2,1)} custom-call(bf16[3,256,256]{2,1,0:T(8,128)(2,1)} %bitcast.4, s32[1,3]{1,0:T(1,128)} %bitcast.5, s32[64,64]{1,0:T(8,128)} %mask.1), custom_call_target="tpu_custom_call" | custom-call | tf_op jit(solution)/shard_map/purify/pallas_call | solution.py:384
  54.3 1.8 %copy.5 = bf16[1,1,3,256,256]{4,3,2,1,0:T(8,128)(2,1)} copy(bf16[1,1,3,256,256]{4,3,2,1,0:T(8,128)(2,1)} %bitcast.3) | data formatting | bytes 786432
where the time goes:
time: 56.2 us; the launch traced here: 56 us
  Pallas kernels  54.3 us (97%)
  local copies, waits for them, and re-layouts  1.77 us (3%)
    pallas_call x1, Pallas kernels, local(): pl.pallas_call(functools.partial(kernel, row_size, col_size), out_shape=j...  54.3 us
    unnamed x1, local copies, waits for them, and re-layouts  1.77 us

commit v1 on v0

--- a/solution.py
+++ b/solution.py
@@ -93,7 +93,7 @@
                 self.beside(step, slot).wait_send()
 
 
-def kernel(
+def dense_kernel(
     row_size, col_size, tiles, ids, mask, out, left, right, squares, square, total, left_ids, right_ids, ids_out,
     left_labels, right_labels, col_sems, square_sems, line_sems, side_sems, row_id_sems, col_id_sems, label_sems,
 ):
@@ -371,43 +371,437 @@
 
     lax.fori_loop(0, length, collect, 0)
 
-
-def solution(mesh):
+X_SLOTS = 3
+Z_SLOTS = 4
+TERMS = 4
+PARTS = 4
+F32, BF16 = jnp.float32, jnp.bfloat16
+
+
+def iota(shape, axis):
+    return lax.broadcasted_iota(jnp.int32, shape, axis)
+
+
+def plan_kernel(row_size, col_size, slots, mask, out, tile_row, tile_col, tile_spot, reach, table, across, stops):
+    blocks, lanes = mask.shape[0], 128
+    block_rows, block_cols = blocks // row_size, blocks // col_size
+    length = row_size // 2
+    lines = 4 * col_size
+    row, col = lax.axis_index("row"), lax.axis_index("col")
+    place, lane = row // 2, lax.rem(row, 2)
+    dot = functools.partial(jnp.dot, preferred_element_type=F32)
+
+    occupied = mask[...].astype(F32)
+    grid = occupied.astype(BF16)
+    row_of, lane_of = iota((blocks, lanes), 0), iota((blocks, lanes), 1)
+    spread = row_of - lax.rem(lane_of, block_cols)
+    keep = lax.rem(row_of, block_rows) == lane_of // block_cols
+    before = (iota((lanes, lanes), 0) <= iota((lanes, lanes), 1)).astype(F32).astype(BF16)
+    region_of, spot_of = iota((row_size, lanes), 0), iota((row_size, lanes), 1)
+    home = spot_of // slots
+    tile_home = iota((1, lanes), 1) // slots
+    spot_value = (spot_of + 1).astype(F32)
+    at = row_of.astype(F32)
+
+    def groups(value):
+        return jnp.sum(value.reshape(row_size, block_rows, lanes), axis=1)
+
+    for panel in range(col_size):
+        pick = (spread == panel * block_cols).astype(F32).astype(BF16)
+        flat = groups(jnp.where(keep, dot(grid, pick), 0.0))
+        rank = dot(flat.astype(BF16), before)
+        spots = jnp.zeros((row_size, lanes), F32)
+        for slot in range(slots):
+            found = jnp.where((rank == slot + 1) & (flat > 0), spot_value, 0.0)
+            found = jnp.sum(found, axis=1, keepdims=True)
+            spots = jnp.where(spot_of == region_of * slots + slot, found, spots)
+        spot = jnp.sum(spots, axis=0, keepdims=True) - 1.0
+        high = jnp.floor((spot + 0.5) / block_cols)
+        block_row = jnp.where(spot >= 0, tile_home.astype(F32) * block_rows + high, -1.0)
+        block_col = jnp.where(spot >= 0, panel * block_cols + spot - high * block_cols, -1.0)
+        tile_spot[pl.ds(panel, 1), :] = spot
+        tile_row[pl.ds(panel, 1), :] = block_row
+        tile_col[pl.ds(panel, 1), :] = block_col
+        by_row = dot(grid, (at == block_row).astype(F32).astype(BF16))
+        by_col = dot(grid, (at == block_col).astype(F32).astype(BF16))
+        wanted = (groups(by_row * by_col) > 0) & (region_of != home)
+        for side in range(2):
+            for way in range(2):
+                step = region_of // 2 + 1 if way == 0 else length - region_of // 2
+                far = jnp.where(wanted & (lax.rem(region_of, 2) == side), step.astype(F32), 0.0)
+                reach[pl.ds((side * 2 + way) * col_size + panel, 1), :] = jnp.max(far, axis=0, keepdims=True)
+
+    far = reach[...]
+    line, tile = iota((lines, lanes), 0), iota((lines, lanes), 1)
+    side, way = line // (2 * col_size), lax.rem(line // col_size, 2)
+    origin, number = tile // slots, lax.rem(tile, slots)
+    begin = jnp.where(way == 0, origin // 2, length - 1 - origin // 2)
+    begin = jnp.minimum(begin, jnp.where(tile < row_size * slots, begin, length))
+    straight = lax.rem(origin, 2) == side
+    crosses = jnp.where((far > 0) & jnp.logical_not(straight), 1.0, 0.0)
+    order = jnp.zeros((lines, lanes), F32)
+    for back in range(1, slots):
+        order += jnp.where(number >= back, pltpu.roll(crosses, back, 1), 0.0)
+    across[...] = jnp.where(crosses > 0, order + 1.0, 0.0)
+    trouble = jnp.where((crosses > 0) & (order >= X_SLOTS - 1), 1.0, 0.0)
+    rank_value = (128 * tile).astype(F32)
+    table_now = jnp.zeros((lines, lanes), F32)
+    stop = jnp.zeros((lines, lanes), F32)
+    number_value = number.astype(F32)
+    for step in range(length - 1):
+        fresh = begin == step
+        ready = jnp.where(fresh, jnp.where(straight, 0.0, order + 1.0), stop)
+        code = jnp.where(
+            fresh, jnp.where(straight, number_value, slots + order), slots + X_SLOTS + stop
+        )
+        left = jnp.where((far > step + 1) & (begin <= step), 1.0, 0.0)
+        key = far * (128 * 128) - rank_value + code + 1.0
+        for turn in range(Z_SLOTS):
+            live = jnp.where((left > 0) & (ready <= turn), key, 0.0)
+            best = jnp.max(live, axis=1, keepdims=True)
+            taken = (live == best) & (live > 0)
+            stop = jnp.where(taken, float(turn), stop)
+            left = jnp.where(taken, 0.0, left)
+            table_now = jnp.where(tile == step * 8 + turn, best, table_now)
+            if turn == Z_SLOTS - 2:
+                trouble = jnp.maximum(trouble, left)
+        trouble = jnp.maximum(trouble, 2.0 * left)
+        stops[step] = stop
+    table_now = table_now - 128 * jnp.floor(table_now / 128)
+    table[...] = jnp.maximum(table_now - 1.0, 0.0)
+
+    here, there = (lane * 2) * col_size + col, (lane * 2 + 1) * col_size + col
+    other = (1 - lane) * 2 * col_size + col
+    tile, tile_number = iota((1, lanes), 1), lax.rem(iota((1, lanes), 1), slots)
+    tile_place = tile_home // 2
+    my_rows, my_cols = tile_row[pl.ds(col, 1), :], tile_col[pl.ds(col, 1), :]
+    beyond = stops[jnp.maximum(place - 1, 0), pl.ds(here, 1), :]
+    under = stops[jnp.maximum(length - 2 - place, 0), pl.ds(there, 1), :]
+    spot = jnp.where(tile_place < place, slots + X_SLOTS + beyond, slots + X_SLOTS + Z_SLOTS + under)
+    spot = jnp.where(tile_place == place, slots - 1 + across[pl.ds(here, 1), :], spot)
+    spot = jnp.where(tile_home == row, tile_number.astype(F32), spot)
+
+    inside = iota((blocks, blocks), 0), iota((blocks, blocks), 1)
+    same_rows = inside[0] // block_rows == inside[1] // block_rows
+    same_cols = inside[0] // block_cols == inside[1] // block_cols
+    lower = (same_rows & (inside[1] < inside[0])).astype(F32).astype(BF16)
+    whole = same_cols.astype(F32).astype(BF16)
+    upper = (same_cols & (inside[0] < inside[1])).astype(F32).astype(BF16)
+    ranks = dot(dot(lower, grid).astype(BF16), whole) + dot(grid, upper)
+    labels = ranks + ((inside[1] // block_cols) * slots).astype(F32)
+    fan = jnp.max(jnp.max(dot(grid, grid) * occupied, axis=1, keepdims=True), axis=0, keepdims=True)
+
+    chosen = (at == my_rows).astype(F32).astype(BF16)
+    met, named = dot(grid, chosen), dot(labels.astype(BF16), chosen)
+    sub = iota((8, lanes), 0)
+    pairs = jnp.zeros((8, lanes), F32)
+    for slot in range(slots):
+        mine = tile == row * slots + slot
+        out_row = jnp.sum(jnp.where(mine, my_rows, 0.0), axis=1, keepdims=True)
+        out_col = jnp.sum(jnp.where(mine, my_cols, 0.0), axis=1, keepdims=True)
+        on_row = at == out_row
+        joins = jnp.sum(jnp.where(on_row, met, 0.0), axis=0, keepdims=True)
+        name = jnp.sum(jnp.where(on_row, named, 0.0), axis=0, keepdims=True)
+        use = (joins > 0) & (my_cols == out_col) & (my_rows >= 0)
+        pairs = jnp.where((sub == slot) & use, name * 64 + spot + 1, pairs)
+    product = jnp.zeros((8, lanes), F32)
+    column = iota((8, lanes), 1)
+    for term in range(TERMS):
+        best = jnp.max(pairs, axis=1, keepdims=True)
+        pairs = jnp.where(pairs == best, 0.0, pairs)
+        product = jnp.where(column == term, best, product)
+
+    level = jnp.max(jnp.max(trouble, axis=1, keepdims=True), axis=0, keepdims=True)
+    level = jnp.where(fan > TERMS, 2.0, level)
+    result = jnp.where(sub == 0, table[pl.ds(here, 1), :], 0.0)
+    result = jnp.where(sub == 1, table[pl.ds(there, 1), :], result)
+    result = jnp.where(sub == 2, across[pl.ds(other, 1), :], result)
+    for slot in range(slots):
+        result = jnp.where(sub == 3 + slot, jnp.sum(jnp.where(sub == slot, product, 0.0), axis=0, keepdims=True), result)
+    result = jnp.where(sub == 6, tile_spot[pl.ds(col, 1), :], result)
+    result = jnp.where(sub == 7, level, result)
+    out[...] = result.astype(jnp.int32)
+
+
+def make_plan(mesh, mask, slots):
+    row_size, col_size = mesh.shape["row"], mesh.shape["col"]
+    panel = pltpu.VMEM((col_size, 128), F32)
+    lines = (4 * col_size, 128)
+    return pl.pallas_call(
+        functools.partial(plan_kernel, row_size, col_size, slots),
+        out_shape=jax.ShapeDtypeStruct((8, 128), jnp.int32),
+        in_specs=[VMEM],
+        out_specs=VMEM,
+        scratch_shapes=[panel, panel, panel] + [pltpu.VMEM(lines, F32)] * 3
+        + [pltpu.VMEM((row_size // 2 - 1, *lines), F32)],
+        name="plan",
+    )(mask)
+
+
+def sparse_kernel(
+    row_size, col_size, x_slots, z_slots, lag, plan, tiles, ids, out, canon, left, held, squares, square, final,
+    x_out, z_out, col_sems, square_sems, x_sems, z_sems,
+):
+    row, col = lax.axis_index("row"), lax.axis_index("col")
+    slots, side = tiles.shape[0], tiles.shape[1]
+    rows = side // PARTS
+    length = row_size // 2
+    place, lane = row // 2, lax.rem(row, 2)
+    mate = row + 1 - 2 * lane
+    chips = col_size // 2
+    chip, core = col // 2, lax.rem(col, 2)
+
+    barrier = pltpu.get_barrier_semaphore()
+
+    def hello(to_row, to_col):
+        pl.semaphore_signal(barrier, inc=1, device_id=(to_row, to_col), device_id_type=MESH)
+
+    hello(mate, col)
+    hello(row, col + 1 - 2 * core)
+    for step in range(1, chips):
+        hello(row, 2 * lax.rem(chip + step, chips) + core)
+    for way in range(2):
+        @pl.when((place + 1 < length) if way == 0 else (place > 0))
+        def _():
+            hello(row + 2 - 4 * way, col)
+
+    for number in range(slots):
+        name = plan[6, row * slots + number]
+        tile = jnp.zeros((side, side), tiles.dtype)
+        for slot in range(slots):
+            tile = jnp.where((ids[0, slot] == name) & (name >= 0), tiles[slot], tile)
+        canon[number] = tile
+    for slot in range(x_slots):
+        tile = canon[0]
+        for number in range(1, slots):
+            tile = jnp.where(plan[2, row * slots + number] == slot + 1, canon[number], tile)
+        x_out[slot] = tile
+
+    ends = jnp.where(place == 0, 1, 0) + jnp.where(place + 1 == length, 1, 0)
+    pl.semaphore_wait(barrier, 2 + chips - 1 + 2 - ends)
+
+    def x_copy(slot, part):
+        span = pl.ds(part * rows, rows)
+        return send(
+            x_out.at[slot, span], held.at[slots + slot, span],
+            x_sems.at[0, slot, part], x_sems.at[1, slot, part], mate, col,
+        )
+
+    def z_copy(way, slot, part):
+        span = pl.ds(part * rows, rows)
+        return send(
+            z_out.at[way, slot, span], held.at[slots + X_SLOTS + way * Z_SLOTS + slot, span],
+            z_sems.at[way, 0, slot, part], z_sems.at[way, 1, slot, part], row + 2 - 4 * way, col,
+        )
+
+    for slot in range(x_slots):
+        for part in range(PARTS):
+            x_copy(slot, part).start()
+    left_gather = ColGather(row, col, col_size, slots, canon, left, col_sems)
+    left_gather.start()
+
+    steps = z_slots * PARTS
+    lead = jnp.where(2 * place < length, 0, 1)
+    hops = jnp.where(lead == 0, place, length - 1 - place)
+    shift = (length - 1 - 2 * hops) * lag
+
+    def hop(way, step, first):
+        slot, part = step // PARTS, lax.rem(step, PARTS)
+        done = jnp.where(way == 0, place, length - 1 - place)
+
+        @pl.when(done + 1 < length)
+        def _():
+            @pl.when(done > 0)
+            def _():
+                z_copy(way, slot, part).wait_recv()
+
+            if first:
+                @pl.when((slot >= 1) & (slot <= x_slots))
+                def _():
+                    x_copy(slot - 1, part).wait_recv()
+
+            span = pl.ds(part * rows, rows)
+            code = plan[way, done * 8 + slot]
+            piece = canon[0, span]
+            for number in range(1, slots):
+                piece = jnp.where(code == number, canon[number, span], piece)
+            z_out[way, slot, span] = piece
+            for other in range(x_slots):
+                @pl.when(other < slot)
+                def _():
+                    z_out[way, slot, span] = jnp.where(
+                        code == slots + other, held[slots + other, span], z_out[way, slot, span]
+                    )
+
+            for other in range(z_slots):
+                @pl.when((other <= slot) & (done > 0))
+                def _():
+                    z_out[way, slot, span] = jnp.where(
+                        code == slots + X_SLOTS + other,
+                        held[slots + X_SLOTS + way * Z_SLOTS + other, span], z_out[way, slot, span],
+                    )
+
+            z_copy(way, slot, part).start()
+
+    def advance(step, unused):
+        @pl.when(step < steps)
+        def _():
+            hop(lead, step, True)
+
+        @pl.when((step >= shift) & (step < steps + shift))
+        def _():
+            hop(1 - lead, step - shift, False)
+
+        return unused
+
+    lax.fori_loop(0, steps + (length - 1) * lag, advance, 0)
+    left_gather.forward()
+
+    for number in range(slots):
+        held[number] = canon[number]
+        left[col, number] = canon[number]
+
+    def arrive(step, unused):
+        slot, part = step // PARTS, lax.rem(step, PARTS)
+        for way in range(2):
+            @pl.when((place + 1 == length) if way == 0 else (place == 0))
+            def _():
+                z_copy(way, slot, part).wait_recv()
+        return unused
+
+    lax.fori_loop(0, steps, arrive, 0)
+    left_gather.collect(None, range(left_gather.chips))
+
+    def sum_terms(panel, number):
+        total = jnp.zeros((side, side), F32)
+        for term in range(TERMS):
+            code = plan[3 + number, term]
+            pair = jnp.maximum(code - 1, 0)
+            name, spot = pair // 64, lax.rem(pair, 64)
+            tile = panel[name // slots, lax.rem(name, slots)]
+            total += jnp.dot(
+                jnp.where(code > 0, tile, jnp.zeros_like(tile)), held[spot], preferred_element_type=F32
+            )
+        return total
+
+    square_gather = ColGather(row, col, col_size, slots, square, squares, square_sems)
+
+    def first(number, unused):
+        tile = sum_terms(left, number).astype(square.dtype)
+        square[number] = tile
+        squares[col, number] = tile
+        for step in range(1, chips):
+            square_gather.across(step, number).start()
+        square_gather.beside(0, number).start()
+        return unused
+
+    lax.fori_loop(0, slots, first, 0)
+    square_gather.forward()
+    square_gather.collect(None, range(chips))
+
+    def second(number, unused):
+        final[number] = (3.0 * square[number].astype(F32) - 2.0 * sum_terms(squares, number)).astype(final.dtype)
+        return unused
+
+    lax.fori_loop(0, slots, second, 0)
+    for slot in range(slots):
+        tile = jnp.zeros((side, side), out.dtype)
+        for number in range(slots):
+            name = plan[6, row * slots + number]
+            tile = jnp.where((ids[0, slot] == name) & (name >= 0), final[number], tile)
+        out[slot] = tile
+
+    left_gather.settle()
+    square_gather.settle()
+
+    def settle_x(step, unused):
+        x_copy(step // PARTS, lax.rem(step, PARTS)).wait_send()
+        return unused
+
+    lax.fori_loop(0, x_slots * PARTS, settle_x, 0)
+
+    def settle_z(step, unused):
+        slot, part = step // PARTS, lax.rem(step, PARTS)
+        for way in range(2):
+            @pl.when((place + 1 < length) if way == 0 else (place > 0))
+            def _():
+                z_copy(way, slot, part).wait_send()
+        return unused
+
+    lax.fori_loop(0, steps, settle_z, 0)
+
+
+def sparse_step(mesh, x_slots, z_slots, barrier_id, plan, stack, ids):
+    row_size, col_size = mesh.shape["row"], mesh.shape["col"]
+    chips = col_size // 2
+    slots, side, _ = stack.shape
+    dma = pltpu.SemaphoreType.DMA
+
+    def tiles(*count):
+        return pltpu.VMEM((*count, side, side), stack.dtype)
+
+    return pl.pallas_call(
+        functools.partial(sparse_kernel, row_size, col_size, x_slots, z_slots, 4),
+        out_shape=jax.ShapeDtypeStruct(stack.shape, stack.dtype),
+        in_specs=[SMEM, VMEM, SMEM],
+        out_specs=VMEM,
+        scratch_shapes=[
+            tiles(slots), tiles(col_size, slots), tiles(slots + X_SLOTS + 2 * Z_SLOTS), tiles(col_size, slots),
+            tiles(slots), tiles(slots), tiles(x_slots), tiles(2, z_slots),
+            dma((4, chips, slots)), dma((4, chips, slots)), dma((2, x_slots, PARTS)), dma((2, 2, z_slots, PARTS)),
+        ],
+        compiler_params=pltpu.CompilerParams(collective_id=barrier_id, has_side_effects=True),
+        name="sparse",
+    )(plan, stack, ids)
+
+
+def dense_step(mesh, stack, ids, mask):
     row_size, col_size = mesh.shape["row"], mesh.shape["col"]
     length, chips = row_size // 2, col_size // 2
     dma = pltpu.SemaphoreType.DMA
-
+    slots, side, _ = stack.shape
+    col_panel = pltpu.VMEM((col_size, slots, side, side), stack.dtype)
+    return pl.pallas_call(
+        functools.partial(dense_kernel, row_size, col_size),
+        out_shape=jax.ShapeDtypeStruct(stack.shape, stack.dtype),
+        in_specs=[VMEM, SMEM, SMEM],
+        out_specs=VMEM,
+        scratch_shapes=[
+            col_panel,
+            pltpu.VMEM((row_size, slots, side, side), stack.dtype),
+            col_panel,
+            pltpu.VMEM(stack.shape, stack.dtype),
+            pltpu.VMEM(stack.shape, jnp.float32),
+            pltpu.VMEM((col_size, 8, 128), jnp.int32),
+            pltpu.VMEM((row_size, 8, 128), jnp.int32),
+            pltpu.VMEM((8, 128), jnp.int32),
+            pltpu.SMEM((col_size, 8, 128), jnp.int32),
+            pltpu.SMEM((row_size, 8, 128), jnp.int32),
+            dma((4, chips, slots)),
+            dma((4, chips, slots)),
+            dma((2, 2, length, slots + 2)),
+            dma((2, length, slots + 1)),
+            dma((2, row_size)),
+            dma((2, col_size)),
+            dma((2,)),
+        ],
+        compiler_params=pltpu.CompilerParams(collective_id=0, has_side_effects=True),
+        name="purify",
+    )(stack, ids, mask)
+
+
+def solution(mesh):
     def local(tiles, stack_index, block_mask):
         stack, ids = tiles[0, 0], stack_index[0]
-        slots, side, _ = stack.shape
-        col_panel = pltpu.VMEM((col_size, slots, side, side), stack.dtype)
-        purified = pl.pallas_call(
-            functools.partial(kernel, row_size, col_size),
-            out_shape=jax.ShapeDtypeStruct(stack.shape, stack.dtype),
-            in_specs=[VMEM, SMEM, SMEM],
-            out_specs=VMEM,
-            scratch_shapes=[
-                col_panel,
-                pltpu.VMEM((row_size, slots, side, side), stack.dtype),
-                col_panel,
-                pltpu.VMEM(stack.shape, stack.dtype),
-                pltpu.VMEM(stack.shape, jnp.float32),
-                pltpu.VMEM((col_size, 8, 128), jnp.int32),
-                pltpu.VMEM((row_size, 8, 128), jnp.int32),
-                pltpu.VMEM((8, 128), jnp.int32),
-                pltpu.SMEM((col_size, 8, 128), jnp.int32),
-                pltpu.SMEM((row_size, 8, 128), jnp.int32),
-                dma((4, chips, slots)),
-                dma((4, chips, slots)),
-                dma((2, 2, length, slots + 2)),
-                dma((2, length, slots + 1)),
-                dma((2, row_size)),
-                dma((2, col_size)),
-                dma((2,)),
-            ],
-            compiler_params=pltpu.CompilerParams(collective_id=0, has_side_effects=True),
-            name="purify",
-        )(stack, ids, block_mask)
+        plan = make_plan(mesh, block_mask, stack.shape[0])
+        purified = lax.switch(
+            plan[7, 0],
+            (
+                lambda: sparse_step(mesh, X_SLOTS - 1, Z_SLOTS - 1, 1, plan, stack, ids),
+                lambda: sparse_step(mesh, X_SLOTS, Z_SLOTS, 2, plan, stack, ids),
+                lambda: dense_step(mesh, stack, ids, block_mask),
+            ),
+        )
         return purified[None, None]
 
     placed = (P("row", "col", None, None, None), P("row", "col", None), P())

time: 56.2 us -> 40.8 us (0.73)
  Pallas kernels: 54.3 us -> 37.7 us
  between operations: 0.01 us -> 0.69 us
    pallas_call x1 -> x2, Pallas kernels: 54.3 us -> 37.7 us  [the longest x1 34.3 us: sparse_step(): pl.pallas_call(functools.partial(sparse_kernel, row_size, col_size, x_slo...]
    unnamed x1 -> x5, local copies, waits for them, and re-layouts: 1.77 us -> 1.39 us
where the time goes in v1:
time: 40.8 us; the launch traced here: 40.5 us
  Pallas kernels  37.7 us (92%)
  local copies, waits for them, and re-layouts  1.91 us (5%)
  between operations  0.69 us (2%)
    pallas_call x1, Pallas kernels, sparse_step(): pl.pallas_call(functools.partial(sparse_kernel, row_size, col_size, x_slo...  34.3 us
    pallas_call x1, Pallas kernels, make_plan(): pl.pallas_call(functools.partial(plan_kernel, row_size, col_size, slots),...  3.4 us
    unnamed x5, local copies, waits for them, and re-layouts  1.39 us

profile of v1, /device:TPU:1, one launch (start us, length us, event | category | flops | bytes accessed | tf_op | source)
XLA Modules:
  0.0 40.5 jit_solution(9823461218010685180)
XLA Ops:
  0.0 0.0 copy-start
  0.0 3.4 %plan.1 = s32[8,128]{1,0:T(8,128)S(1)} custom-call(s32[64,64]{1,0:T(8,128)} %mask.1), custom_call_target="tpu_custom_call" | custom-call | tf_op jit(solution)/shard_map/plan/pallas_call | solution.py:530
  3.4 0.5 %slice.3 = s32[1,1]{1,0:T(1,128)} slice(s32[8,128]{1,0:T(8,128)S(1)} %plan.1), slice={[7:8], [0:1]} | slice | bytes 8 | tf_op jit(solution)/shard_map/slice | solution.py:798
  4.6 0.0 copy-start.1
  4.6 0.0 copy-done
  4.6 0.6 %copy-done.1 = s32[1,1,3]{2,1,0:T(1,128)S(1)} copy-done((s32[1,1,3]{2,1,0:T(1,128)S(1)}, s32[1,1,3]{2,1,0:T(1,128)}, u32[]{:S(2)}) %copy-start.1) | copy-done | bytes 36
  5.2 34.5 %conditional.1 = (bf16[1,1,3,256,256]{4,3,2,1,0:T(8,128)(2,1)S(1)}) conditional(s32[]{:T(128)} %bitcast.3, (s32[8,128]{1,0:T(8,128)S(1)}, bf16[3,256,256]{2,1,0:T(8,128)(2,1)}, s32[1,3]{1,0:T(1,128)S(1)}) %tuple.29, (s32[8,128]{1,0:T(8,128)S(1)}, bf16[3,256,256]{2,1,0:T(8,128)(2,1)}, s32[1,3]{1,0:T(1,128)S(1)}) %tuple.30, ...), branch_computations={%region_0.0_spmd, %region_1.0_spmd, %region_2.0_spmd} | conditional | bytes 8 | solution.py:797
  5.2 34.3 %sparse.2 = bf16[3,256,256]{2,1,0:T(8,128)(2,1)S(1)} custom-call(s32[8,128]{1,0:T(8,128)S(1)} %get-tuple-element.28.plan, bf16[3,256,256]{2,1,0:T(8,128)(2,1)} %get-tuple-element.29.tiles, s32[1,3]{1,0:T(1,128)S(1)} %get-tuple-element.30.ids), custom_call_target="tpu_custom_call" | custom-call | tf_op jit(solution)/shard_map/cond/branch_0_fun/sparse/pallas_call | solution.py:743
  39.8 0.7 %copy.11 = bf16[1,1,3,256,256]{4,3,2,1,0:T(8,128)(2,1)} copy(bf16[1,1,3,256,256]{4,3,2,1,0:T(8,128)(2,1)S(1)} %get-tuple-element.37) | data formatting | bytes 786432
Async XLA Ops:
  0.0 4.6 %copy-start = (s32[64,64]{1,0:T(8,128)S(1)}, s32[64,64]{1,0:T(8,128)}, u32[]{:S(2)}) copy-start(s32[64,64]{1,0:T(8,128)} %mask.1) | copy-start | bytes 49156
  4.6 0.7 %copy-start.1 = (s32[1,1,3]{2,1,0:T(1,128)S(1)}, s32[1,1,3]{2,1,0:T(1,128)}, u32[]{:S(2)}) copy-start(s32[1,1,3]{2,1,0:T(1,128)} %param.7) | copy-start | bytes 40

commit v2 on v1

--- a/solution.py
+++ b/solution.py
@@ -6,10 +6,12 @@
 from jax.experimental import pallas as pl
 from jax.experimental.pallas import tpu as pltpu
 from jax.sharding import PartitionSpec as P
+from jax._src.lax.control_flow.conditionals import _switch_internal
 
 MESH = pl.DeviceIdType.MESH
 VMEM = pl.BlockSpec(memory_space=pltpu.VMEM)
 SMEM = pl.BlockSpec(memory_space=pltpu.SMEM)
+HBM = pl.BlockSpec(memory_space=pltpu.HBM)
 
 
 def send(src, dst, send_sem, recv_sem, row, col):
@@ -38,9 +40,11 @@
 
 
 class ColGather:
-    def __init__(self, row, col, col_size, slots, own, panel, sems):
+    def __init__(self, row, col, col_size, slots, own, panel, sems, far=None, far_slots=None):
         self.row, self.col, self.slots = row, col, slots
         self.own, self.panel, self.sems = own, panel, sems
+        self.far = own if far is None else far
+        self.far_slots = slots if far_slots is None else far_slots
         self.chips = col_size // 2
         self.chip, self.core = col // 2, lax.rem(col, 2)
         self.partner = col + 1 - 2 * self.core
@@ -48,7 +52,7 @@
     def across(self, step, slot):
         target = 2 * lax.rem(self.chip + step, self.chips) + self.core
         return send(
-            self.own.at[slot], self.panel.at[self.col, slot],
+            self.far.at[slot], self.panel.at[self.col, slot],
             self.sems.at[0, step - 1, slot], self.sems.at[1, step - 1, slot], self.row, target,
         )
 
@@ -71,23 +75,26 @@
         return 2 * lax.rem(self.chip + self.chips - step, self.chips) + core
 
     def forward(self, use=None):
-        for slot in range(self.slots):
+        for slot in range(self.far_slots):
             for step in range(1, self.chips):
                 self.across(step, slot).wait_recv()
                 self.beside(step, slot).start()
                 if use is not None:
                     use(self.origin(step, self.core), slot)
 
+    def count(self, step):
+        return self.far_slots if step else self.slots
+
     def collect(self, use, steps):
         for step in steps:
-            for slot in range(self.slots):
+            for slot in range(self.count(step)):
                 self.beside(step, slot).wait_recv()
                 if use is not None:
                     use(self.origin(step, 1 - self.core), slot)
 
     def settle(self):
         for step in range(self.chips):
-            for slot in range(self.slots):
+            for slot in range(self.count(step)):
                 if step:
                     self.across(step, slot).wait_send()
                 self.beside(step, slot).wait_send()
@@ -107,7 +114,7 @@
     lane_iota = lax.broadcasted_iota(jnp.int32, (8, 128), 1)
     packed = jnp.full((8, 128), -1, jnp.int32)
     for slot in range(slots):
-        packed = jnp.where(lane_iota == slot, ids[0, slot], packed)
+        packed = jnp.where(lane_iota == slot, ids[7, slot], packed)
     ids_out[...] = packed
     greet(row_size, col_size, row, col, True)
 
@@ -239,7 +246,7 @@
     block_rows, block_cols = mask.shape[0] // row_size, mask.shape[1] // col_size
     owns = []
     for slot in range(slots):
-        own = ids[0, slot]
+        own = ids[7, slot]
         own_row, own_col = own // block_cols, lax.rem(own, block_cols)
         out_row, out_col = row * block_rows + own_row, col * block_cols + own_col
         owns.append((own_row, own_col, out_row, out_col, mask[out_row, out_col] > 0))
@@ -372,7 +379,8 @@
     lax.fori_loop(0, length, collect, 0)
 
 X_SLOTS = 3
-Z_SLOTS = 4
+Z_SLOTS = 5
+Y_SLOTS = 2
 TERMS = 4
 PARTS = 4
 F32, BF16 = jnp.float32, jnp.bfloat16
@@ -382,7 +390,16 @@
     return lax.broadcasted_iota(jnp.int32, shape, axis)
 
 
-def plan_kernel(row_size, col_size, slots, mask, out, tile_row, tile_col, tile_spot, reach, table, across, stops):
+def plan_kernel(
+    row_size, col_size, slots, far_ids, far_mask, far_tiles, out, choice, canon, x_out, ids, mask, tiles, tile_row,
+    tile_col, tile_spot, reach, ranges, table, across, stops, sems,
+):
+    fetches = [
+        pltpu.make_async_copy(src, dst, sems.at[number])
+        for number, (src, dst) in enumerate(((far_mask, mask), (far_ids, ids), (far_tiles, tiles)))
+    ]
+    for fetch in fetches:
+        fetch.start()
     blocks, lanes = mask.shape[0], 128
     block_rows, block_cols = blocks // row_size, blocks // col_size
     length = row_size // 2
@@ -391,6 +408,7 @@
     place, lane = row // 2, lax.rem(row, 2)
     dot = functools.partial(jnp.dot, preferred_element_type=F32)
 
+    fetches[0].wait()
     occupied = mask[...].astype(F32)
     grid = occupied.astype(BF16)
     row_of, lane_of = iota((blocks, lanes), 0), iota((blocks, lanes), 1)
@@ -430,6 +448,11 @@
                 step = region_of // 2 + 1 if way == 0 else length - region_of // 2
                 far = jnp.where(wanted & (lax.rem(region_of, 2) == side), step.astype(F32), 0.0)
                 reach[pl.ds((side * 2 + way) * col_size + panel, 1), :] = jnp.max(far, axis=0, keepdims=True)
+            gap = jnp.abs(region_of // 2 - home // 2) + 1
+            gap = jnp.where(wanted & (lax.rem(region_of, 2) == side), gap.astype(F32), 0.0)
+            gap = jnp.max(gap, axis=0, keepdims=True)
+            for way in range(2):
+                ranges[pl.ds((side * 2 + way) * col_size + panel, 1), :] = gap
 
     far = reach[...]
     line, tile = iota((lines, lanes), 0), iota((lines, lanes), 1)
@@ -438,19 +461,21 @@
     begin = jnp.where(way == 0, origin // 2, length - 1 - origin // 2)
     begin = jnp.minimum(begin, jnp.where(tile < row_size * slots, begin, length))
     straight = lax.rem(origin, 2) == side
-    crosses = jnp.where((far > 0) & jnp.logical_not(straight), 1.0, 0.0)
+    crosses = (ranges[...] > 0) & jnp.logical_not(straight)
+    value = jnp.where(crosses, ranges[...] * 8 - number.astype(F32), -8.0)
     order = jnp.zeros((lines, lanes), F32)
     for back in range(1, slots):
-        order += jnp.where(number >= back, pltpu.roll(crosses, back, 1), 0.0)
-    across[...] = jnp.where(crosses > 0, order + 1.0, 0.0)
-    trouble = jnp.where((crosses > 0) & (order >= X_SLOTS - 1), 1.0, 0.0)
+        order += jnp.where((number >= back) & (pltpu.roll(value, back, 1) > value), 1.0, 0.0)
+        order += jnp.where((number + back < slots) & (pltpu.roll(value, lanes - back, 1) > value), 1.0, 0.0)
+    across[...] = jnp.where(crosses, order + 1.0, 0.0)
+    trouble = jnp.zeros((lines, lanes), F32)
     rank_value = (128 * tile).astype(F32)
     table_now = jnp.zeros((lines, lanes), F32)
     stop = jnp.zeros((lines, lanes), F32)
     number_value = number.astype(F32)
     for step in range(length - 1):
         fresh = begin == step
-        ready = jnp.where(fresh, jnp.where(straight, 0.0, order + 1.0), stop)
+        ready = jnp.where(fresh, jnp.where(straight, 0.0, order + 1.0), stop + 1.0)
         code = jnp.where(
             fresh, jnp.where(straight, number_value, slots + order), slots + X_SLOTS + stop
         )
@@ -487,14 +512,37 @@
     lower = (same_rows & (inside[1] < inside[0])).astype(F32).astype(BF16)
     whole = same_cols.astype(F32).astype(BF16)
     upper = (same_cols & (inside[0] < inside[1])).astype(F32).astype(BF16)
+    chip_of = inside[1] // (2 * block_cols)
+    flipped = occupied.T.astype(BF16)
+    shared = dot(grid, flipped)
+    inner = jnp.zeros((blocks, blocks), F32)
+    for chip in range(col_size // 2):
+        on_chip = jnp.where(chip_of == chip, occupied, 0.0).astype(BF16)
+        inner = jnp.where(chip_of == chip, dot(on_chip, flipped), inner)
+    leaves = jnp.where((occupied > 0) & (shared > inner), 1.0, 0.0)
+    gone = leaves.astype(BF16)
     ranks = dot(dot(lower, grid).astype(BF16), whole) + dot(grid, upper)
-    labels = ranks + ((inside[1] // block_cols) * slots).astype(F32)
-    fan = jnp.max(jnp.max(dot(grid, grid) * occupied, axis=1, keepdims=True), axis=0, keepdims=True)
+    y_ranks = dot(dot(lower, gone).astype(BF16), whole) + dot(gone, upper)
+    panels = ((inside[1] // block_cols) * slots).astype(F32)
+    labels = ranks + panels
+    y_labels = jnp.where(chip_of == col // 2, ranks, y_ranks) + panels
+    y_order = leaves * (y_ranks + 1.0)
+
+    def peak(value):
+        return jnp.max(jnp.max(value, axis=1, keepdims=True), axis=0, keepdims=True)
+
+    fan = peak(dot(grid, grid) * occupied)
+    crowd = peak(y_order)
 
     chosen = (at == my_rows).astype(F32).astype(BF16)
-    met, named = dot(grid, chosen), dot(labels.astype(BF16), chosen)
-    sub = iota((8, lanes), 0)
+    met = dot(grid, chosen)
+    named, y_named = dot(labels.astype(BF16), chosen), dot(y_labels.astype(BF16), chosen)
+    sub, column = iota((8, lanes), 0), iota((8, lanes), 1)
     pairs = jnp.zeros((8, lanes), F32)
+    fetches[1].wait()
+    result = jnp.where(sub == 0, table[pl.ds(here, 1), :], 0.0)
+    result = jnp.where(sub == 1, table[pl.ds(there, 1), :], result)
+    inside_rows, inside_cols = inside[0].astype(F32), inside[1].astype(F32)
     for slot in range(slots):
         mine = tile == row * slots + slot
         out_row = jnp.sum(jnp.where(mine, my_rows, 0.0), axis=1, keepdims=True)
@@ -502,54 +550,87 @@
         on_row = at == out_row
         joins = jnp.sum(jnp.where(on_row, met, 0.0), axis=0, keepdims=True)
         name = jnp.sum(jnp.where(on_row, named, 0.0), axis=0, keepdims=True)
+        y_name = jnp.sum(jnp.where(on_row, y_named, 0.0), axis=0, keepdims=True)
         use = (joins > 0) & (my_cols == out_col) & (my_rows >= 0)
         pairs = jnp.where((sub == slot) & use, name * 64 + spot + 1, pairs)
+        pairs = jnp.where((sub == slot + slots) & use, y_name * 64 + spot + 1, pairs)
+        y_spot = jnp.where((inside_rows == out_row) & (inside_cols == out_col), y_order, 0.0)
+        y_spot = jnp.sum(jnp.sum(y_spot, axis=1, keepdims=True), axis=0, keepdims=True)
+        result = jnp.where((sub == 6) & (column == 8 + slot), y_spot, result)
     product = jnp.zeros((8, lanes), F32)
-    column = iota((8, lanes), 1)
+    shifted = column - jnp.where(sub >= slots, 16, 0)
     for term in range(TERMS):
         best = jnp.max(pairs, axis=1, keepdims=True)
         pairs = jnp.where(pairs == best, 0.0, pairs)
-        product = jnp.where(column == term, best, product)
-
-    level = jnp.max(jnp.max(trouble, axis=1, keepdims=True), axis=0, keepdims=True)
-    level = jnp.where(fan > TERMS, 2.0, level)
-    result = jnp.where(sub == 0, table[pl.ds(here, 1), :], 0.0)
-    result = jnp.where(sub == 1, table[pl.ds(there, 1), :], result)
-    result = jnp.where(sub == 2, across[pl.ds(other, 1), :], result)
+        product = jnp.where(shifted == term, best, product)
+
+    level = peak(trouble) * 2.0
+    level = jnp.where(fan > TERMS, 4.0, level) + jnp.where((level < 4) & (fan <= TERMS) & (crowd > Y_SLOTS), 1.0, 0.0)
+    choice[...] = level.astype(jnp.int32)
     for slot in range(slots):
-        result = jnp.where(sub == 3 + slot, jnp.sum(jnp.where(sub == slot, product, 0.0), axis=0, keepdims=True), result)
-    result = jnp.where(sub == 6, tile_spot[pl.ds(col, 1), :], result)
-    result = jnp.where(sub == 7, level, result)
+        mine = (tile_home == row) & (tile_spot[pl.ds(col, 1), :] == ids[0, slot].astype(F32))
+        match = jnp.sum(jnp.where(mine, tile_number.astype(F32) + 1.0, 0.0), axis=1, keepdims=True)
+        order = jnp.where(tile == row * slots + slot, across[pl.ds(other, 1), :], 0.0)
+        order = jnp.sum(order, axis=1, keepdims=True)
+        result = jnp.where((sub == 6) & (column == slot), match, result)
+        result = jnp.where((sub == 2) & (column == slot), order, result)
+        result = jnp.where((sub == 7) & (column == slot), ids[0, slot].astype(F32), result)
+        both = jnp.where((sub == slot) | (sub == slot + slots), product, 0.0)
+        result = jnp.where(sub == 3 + slot, jnp.sum(both, axis=0, keepdims=True), result)
     out[...] = result.astype(jnp.int32)
 
-
-def make_plan(mesh, mask, slots):
+    fetches[2].wait()
+    held = [[result[6:7, slot : slot + 1] == number + 1 for slot in range(slots)] for number in range(slots)]
+    for number in range(slots):
+        piece = jnp.zeros(tiles.shape[1:], tiles.dtype)
+        for slot in range(slots):
+            piece = jnp.where(held[number][slot], tiles[slot], piece)
+        canon[number] = piece
+    for slot in range(slots):
+        piece = canon[0]
+        for number in range(1, slots):
+            piece = jnp.where(result[2:3, number : number + 1] == slot + 1, canon[number], piece)
+        x_out[slot] = piece
+
+
+def make_plan(mesh, ids, mask, stack):
     row_size, col_size = mesh.shape["row"], mesh.shape["col"]
+    slots = ids.shape[1]
     panel = pltpu.VMEM((col_size, 128), F32)
     lines = (4 * col_size, 128)
     return pl.pallas_call(
         functools.partial(plan_kernel, row_size, col_size, slots),
-        out_shape=jax.ShapeDtypeStruct((8, 128), jnp.int32),
-        in_specs=[VMEM],
-        out_specs=VMEM,
-        scratch_shapes=[panel, panel, panel] + [pltpu.VMEM(lines, F32)] * 3
-        + [pltpu.VMEM((row_size // 2 - 1, *lines), F32)],
+        out_shape=(
+            jax.ShapeDtypeStruct((8, 128), jnp.int32),
+            jax.ShapeDtypeStruct((1, 1), jnp.int32),
+            jax.ShapeDtypeStruct(stack.shape, stack.dtype),
+            jax.ShapeDtypeStruct(stack.shape, stack.dtype),
+        ),
+        in_specs=[HBM, HBM, HBM],
+        out_specs=(VMEM, VMEM, VMEM, VMEM),
+        scratch_shapes=[
+            pltpu.SMEM(ids.shape, ids.dtype), pltpu.VMEM(mask.shape, mask.dtype), pltpu.VMEM(stack.shape, stack.dtype),
+            panel, panel, panel, *[pltpu.VMEM(lines, F32)] * 4, pltpu.VMEM((row_size // 2 - 1, *lines), F32),
+            pltpu.SemaphoreType.DMA((3,)),
+        ],
+        compiler_params=pltpu.CompilerParams(vmem_limit_bytes=16 * 2**20),
         name="plan",
-    )(mask)
+    )(ids, mask, stack)
 
 
 def sparse_kernel(
-    row_size, col_size, x_slots, z_slots, lag, plan, tiles, ids, out, canon, left, held, squares, square, final,
-    x_out, z_out, col_sems, square_sems, x_sems, z_sems,
+    row_size, col_size, z_slots, y_slots, plan, canon, x_out, out, left, held, squares, square, final,
+    y_out, z_out, col_sems, square_sems, x_sems, z_sems,
 ):
     row, col = lax.axis_index("row"), lax.axis_index("col")
-    slots, side = tiles.shape[0], tiles.shape[1]
+    slots, side = canon.shape[0], canon.shape[1]
     rows = side // PARTS
     length = row_size // 2
     place, lane = row // 2, lax.rem(row, 2)
     mate = row + 1 - 2 * lane
     chips = col_size // 2
     chip, core = col // 2, lax.rem(col, 2)
+    x_slots = slots
 
     barrier = pltpu.get_barrier_semaphore()
 
@@ -565,18 +646,6 @@
         def _():
             hello(row + 2 - 4 * way, col)
 
-    for number in range(slots):
-        name = plan[6, row * slots + number]
-        tile = jnp.zeros((side, side), tiles.dtype)
-        for slot in range(slots):
-            tile = jnp.where((ids[0, slot] == name) & (name >= 0), tiles[slot], tile)
-        canon[number] = tile
-    for slot in range(x_slots):
-        tile = canon[0]
-        for number in range(1, slots):
-            tile = jnp.where(plan[2, row * slots + number] == slot + 1, canon[number], tile)
-        x_out[slot] = tile
-
     ends = jnp.where(place == 0, 1, 0) + jnp.where(place + 1 == length, 1, 0)
     pl.semaphore_wait(barrier, 2 + chips - 1 + 2 - ends)
 
@@ -600,82 +669,69 @@
     left_gather = ColGather(row, col, col_size, slots, canon, left, col_sems)
     left_gather.start()
 
-    steps = z_slots * PARTS
-    lead = jnp.where(2 * place < length, 0, 1)
-    hops = jnp.where(lead == 0, place, length - 1 - place)
-    shift = (length - 1 - 2 * hops) * lag
-
-    def hop(way, step, first):
-        slot, part = step // PARTS, lax.rem(step, PARTS)
-        done = jnp.where(way == 0, place, length - 1 - place)
-
-        @pl.when(done + 1 < length)
-        def _():
-            @pl.when(done > 0)
+    done = (place, length - 1 - place)
+    for slot in range(z_slots):
+        for way in range(2):
+            @pl.when(done[way] + 1 < length)
             def _():
-                z_copy(way, slot, part).wait_recv()
-
-            if first:
-                @pl.when((slot >= 1) & (slot <= x_slots))
+                code = plan[way, done[way] * 8 + slot]
+                tile = canon[0]
+                for number in range(1, slots):
+                    tile = jnp.where(code == number, canon[number], tile)
+                for other in range(min(slot - 1, x_slots)):
+                    tile = jnp.where(code == slots + other, held[slots + other], tile)
+                for other in range(slot - 1):
+                    spot = X_SLOTS + slots + other
+                    tile = jnp.where(code == spot, held[spot + way * Z_SLOTS], tile)
+                z_out[way, slot] = tile
+
+        for part in range(PARTS):
+            span = pl.ds(part * rows, rows)
+            if 1 <= slot <= x_slots:
+                x_copy(slot - 1, part).wait_recv()
+            for way in range(2):
+                @pl.when(done[way] + 1 < length)
                 def _():
-                    x_copy(slot - 1, part).wait_recv()
-
-            span = pl.ds(part * rows, rows)
-            code = plan[way, done * 8 + slot]
-            piece = canon[0, span]
-            for number in range(1, slots):
-                piece = jnp.where(code == number, canon[number, span], piece)
-            z_out[way, slot, span] = piece
-            for other in range(x_slots):
-                @pl.when(other < slot)
-                def _():
-                    z_out[way, slot, span] = jnp.where(
-                        code == slots + other, held[slots + other, span], z_out[way, slot, span]
-                    )
-
-            for other in range(z_slots):
-                @pl.when((other <= slot) & (done > 0))
-                def _():
-                    z_out[way, slot, span] = jnp.where(
-                        code == slots + X_SLOTS + other,
-                        held[slots + X_SLOTS + way * Z_SLOTS + other, span], z_out[way, slot, span],
-                    )
-
-            z_copy(way, slot, part).start()
-
-    def advance(step, unused):
-        @pl.when(step < steps)
-        def _():
-            hop(lead, step, True)
-
-        @pl.when((step >= shift) & (step < steps + shift))
-        def _():
-            hop(1 - lead, step - shift, False)
-
-        return unused
-
-    lax.fori_loop(0, steps + (length - 1) * lag, advance, 0)
+                    if slot:
+                        @pl.when(done[way] > 0)
+                        def _():
+                            z_copy(way, slot - 1, part).wait_recv()
+
+                        code = plan[way, done[way] * 8 + slot]
+                        piece = z_out[way, slot, span]
+                        if slot <= x_slots:
+                            piece = jnp.where(code == slots + slot - 1, held[slots + slot - 1, span], piece)
+                        spot = X_SLOTS + slots + slot - 1
+                        piece = jnp.where(code == spot, held[spot + way * Z_SLOTS, span], piece)
+                        z_out[way, slot, span] = piece
+                    z_copy(way, slot, part).start()
+
     left_gather.forward()
-
     for number in range(slots):
         held[number] = canon[number]
         left[col, number] = canon[number]
 
-    def arrive(step, unused):
-        slot, part = step // PARTS, lax.rem(step, PARTS)
-        for way in range(2):
-            @pl.when((place + 1 == length) if way == 0 else (place == 0))
-            def _():
-                z_copy(way, slot, part).wait_recv()
-        return unused
-
-    lax.fori_loop(0, steps, arrive, 0)
+    for slot in range(z_slots - 1, x_slots):
+        for part in range(PARTS):
+            x_copy(slot, part).wait_recv()
+    for way in range(2):
+        @pl.when(done[way] + 1 == length)
+        def _():
+            for slot in range(z_slots - 1):
+                for part in range(PARTS):
+                    z_copy(way, slot, part).wait_recv()
+
+        @pl.when(done[way] > 0)
+        def _():
+            for part in range(PARTS):
+                z_copy(way, z_slots - 1, part).wait_recv()
+
     left_gather.collect(None, range(left_gather.chips))
 
-    def sum_terms(panel, number):
+    def sum_terms(panel, number, first):
         total = jnp.zeros((side, side), F32)
         for term in range(TERMS):
-            code = plan[3 + number, term]
+            code = plan[3 + number, first + term]
             pair = jnp.maximum(code - 1, 0)
             name, spot = pair // 64, lax.rem(pair, 64)
             tile = panel[name // slots, lax.rem(name, slots)]
@@ -684,14 +740,20 @@
             )
         return total
 
-    square_gather = ColGather(row, col, col_size, slots, square, squares, square_sems)
+    square_gather = ColGather(row, col, col_size, slots, square, squares, square_sems, y_out, y_slots)
+
+    for slot in range(y_slots):
+        number = jnp.int32(0)
+        for other in range(1, slots):
+            number = jnp.where(plan[6, 8 + other] == slot + 1, other, number)
+        y_out[slot] = sum_terms(left, number, 0).astype(square.dtype)
+        for step in range(1, chips):
+            square_gather.across(step, slot).start()
 
     def first(number, unused):
-        tile = sum_terms(left, number).astype(square.dtype)
+        tile = sum_terms(left, number, 0).astype(square.dtype)
         square[number] = tile
         squares[col, number] = tile
-        for step in range(1, chips):
-            square_gather.across(step, number).start()
         square_gather.beside(0, number).start()
         return unused
 
@@ -700,38 +762,35 @@
     square_gather.collect(None, range(chips))
 
     def second(number, unused):
-        final[number] = (3.0 * square[number].astype(F32) - 2.0 * sum_terms(squares, number)).astype(final.dtype)
+        final[number] = (3.0 * square[number].astype(F32) - 2.0 * sum_terms(squares, number, 16)).astype(final.dtype)
         return unused
 
     lax.fori_loop(0, slots, second, 0)
     for slot in range(slots):
         tile = jnp.zeros((side, side), out.dtype)
         for number in range(slots):
-            name = plan[6, row * slots + number]
-            tile = jnp.where((ids[0, slot] == name) & (name >= 0), final[number], tile)
+            tile = jnp.where(plan[6, slot] == number + 1, final[number], tile)
         out[slot] = tile
 
     left_gather.settle()
     square_gather.settle()
 
-    def settle_x(step, unused):
-        x_copy(step // PARTS, lax.rem(step, PARTS)).wait_send()
-        return unused
-
-    lax.fori_loop(0, x_slots * PARTS, settle_x, 0)
-
-    def settle_z(step, unused):
-        slot, part = step // PARTS, lax.rem(step, PARTS)
-        for way in range(2):
-            @pl.when((place + 1 < length) if way == 0 else (place > 0))
-            def _():
-                z_copy(way, slot, part).wait_send()
-        return unused
-
-    lax.fori_loop(0, steps, settle_z, 0)
-
-
-def sparse_step(mesh, x_slots, z_slots, barrier_id, plan, stack, ids):
+    for part in range(PARTS):
+        for slot in range(x_slots):
+            x_copy(slot, part).wait_send()
+    for way in range(2):
+        @pl.when(done[way] + 1 < length)
+        def _():
+            for slot in range(z_slots):
+                for part in range(PARTS):
+                    z_copy(way, slot, part).wait_send()
+
+
+def room(panels, slots, side):
+    return (4 * panels + 16) * slots * side * side * 2 + 8 * 2**20
+
+
+def sparse_step(mesh, z_slots, y_slots, barrier_id, plan, stack, x_stack):
     row_size, col_size = mesh.shape["row"], mesh.shape["col"]
     chips = col_size // 2
     slots, side, _ = stack.shape
@@ -741,21 +800,23 @@
         return pltpu.VMEM((*count, side, side), stack.dtype)
 
     return pl.pallas_call(
-        functools.partial(sparse_kernel, row_size, col_size, x_slots, z_slots, 4),
+        functools.partial(sparse_kernel, row_size, col_size, z_slots, y_slots),
         out_shape=jax.ShapeDtypeStruct(stack.shape, stack.dtype),
-        in_specs=[SMEM, VMEM, SMEM],
+        in_specs=[SMEM, VMEM, VMEM],
         out_specs=VMEM,
         scratch_shapes=[
-            tiles(slots), tiles(col_size, slots), tiles(slots + X_SLOTS + 2 * Z_SLOTS), tiles(col_size, slots),
-            tiles(slots), tiles(slots), tiles(x_slots), tiles(2, z_slots),
-            dma((4, chips, slots)), dma((4, chips, slots)), dma((2, x_slots, PARTS)), dma((2, 2, z_slots, PARTS)),
+            tiles(col_size, slots), tiles(slots + X_SLOTS + 2 * Z_SLOTS), tiles(col_size, slots),
+            tiles(slots), tiles(slots), tiles(y_slots), tiles(2, z_slots),
+            dma((4, chips, slots)), dma((4, chips, slots)), dma((2, slots, PARTS)), dma((2, 2, z_slots, PARTS)),
         ],
-        compiler_params=pltpu.CompilerParams(collective_id=barrier_id, has_side_effects=True),
+        compiler_params=pltpu.CompilerParams(
+            collective_id=barrier_id, has_side_effects=True, vmem_limit_bytes=room(col_size, slots, side)
+        ),
         name="sparse",
-    )(plan, stack, ids)
-
-
-def dense_step(mesh, stack, ids, mask):
+    )(plan, stack, x_stack)
+
+
+def dense_step(mesh, plan, stack, mask):
     row_size, col_size = mesh.shape["row"], mesh.shape["col"]
     length, chips = row_size // 2, col_size // 2
     dma = pltpu.SemaphoreType.DMA
@@ -785,23 +846,24 @@
             dma((2, col_size)),
             dma((2,)),
         ],
-        compiler_params=pltpu.CompilerParams(collective_id=0, has_side_effects=True),
+        compiler_params=pltpu.CompilerParams(
+            collective_id=0, has_side_effects=True, vmem_limit_bytes=room(row_size + col_size, slots, side)
+        ),
         name="purify",
-    )(stack, ids, mask)
+    )(stack, plan, mask)
 
 
 def solution(mesh):
     def local(tiles, stack_index, block_mask):
-        stack, ids = tiles[0, 0], stack_index[0]
-        plan = make_plan(mesh, block_mask, stack.shape[0])
-        purified = lax.switch(
-            plan[7, 0],
-            (
-                lambda: sparse_step(mesh, X_SLOTS - 1, Z_SLOTS - 1, 1, plan, stack, ids),
-                lambda: sparse_step(mesh, X_SLOTS, Z_SLOTS, 2, plan, stack, ids),
-                lambda: dense_step(mesh, stack, ids, block_mask),
-            ),
-        )
+        stack = tiles[0, 0]
+        plan, choice, canon, crossing = make_plan(mesh, stack_index[0], block_mask, stack)
+        branches = [
+            functools.partial(sparse_step, mesh, z_slots, y_slots, 1 + 2 * (z_slots == Z_SLOTS) + (y_slots > Y_SLOTS))
+            for z_slots in (Z_SLOTS - 1, Z_SLOTS) for y_slots in (Y_SLOTS, stack.shape[0])
+        ]
+        branches = [lambda branch=branch: branch(plan, canon, crossing) for branch in branches]
+        branches.append(lambda: dense_step(mesh, plan, stack, block_mask))
+        purified = _switch_internal(choice[0, 0], branches, (), branches_platforms=None)
         return purified[None, None]
 
     placed = (P("row", "col", None, None, None), P("row", "col", None), P())

time: 40.8 us -> 35.9 us (0.88)
  Pallas kernels: 37.7 us -> 33.4 us
  loops' own time: 0.23 us -> 0.9 us
  between operations: 0.69 us -> 0.04 us
  local copies, waits for them, and re-layouts: 1.91 us -> 1.41 us
    pallas_call x1, Pallas kernels: 34.3 us -> 29.1 us  [sparse_step(): pl.pallas_call(functools.partial(sparse_kernel, row_size, col_size, z_slo...]
    pallas_call x1, Pallas kernels: 3.4 us -> 4.34 us  [make_plan(): pl.pallas_call(functools.partial(plan_kernel, row_size, col_size, slots),...]
    another operation x1, loops' own time: 0.23 us -> 0.9 us  [local(): _switch_internal(choice[0, 0], branches, (), branches_platforms=None)]
    slice x1 -> x0, local copies, waits for them, and re-layouts: 0.52 us -> none  [local(): plan[7, 0]]
    unnamed x5 -> x7, local copies, waits for them, and re-layouts: 1.39 us -> 1.41 us
where the time goes in v2:
time: 35.9 us; the launch traced here: 35.8 us
  Pallas kernels  33.4 us (93%)
  local copies, waits for them, and re-layouts  1.41 us (4%)
  loops' own time  0.9 us (3%)
    pallas_call x1, Pallas kernels, sparse_step(): pl.pallas_call(functools.partial(sparse_kernel, row_size, col_size, z_slo...  29.1 us
    pallas_call x1, Pallas kernels, make_plan(): pl.pallas_call(functools.partial(plan_kernel, row_size, col_size, slots),...  4.34 us
    unnamed x7, local copies, waits for them, and re-layouts  1.41 us
    another operation x1, loops' own time, local(): _switch_internal(choice[0, 0], branches, (), branches_platforms=None)  0.9 us

profile of v2, /device:TPU:1, one launch (start us, length us, event | category | flops | bytes accessed | tf_op | source)
XLA Modules:
  0.0 35.8 jit_solution(2088530836194015315)
XLA Ops:
  0.0 0.0 copy-start
  0.0 0.0 copy-start.1
  0.0 0.7 %copy-done = s32[1,1,3]{2,1,0:T(1,128)S(1)} copy-done((s32[1,1,3]{2,1,0:T(1,128)S(1)}, s32[1,1,3]{2,1,0:T(1,128)}, u32[]{:S(2)}) %copy-start) | copy-done | bytes 36
  0.7 0.0 copy-start.2
  0.7 4.3 %plan.1 = (s32[8,128]{1,0:T(8,128)S(1)}, s32[1,1]{1,0:T(1,128)}, bf16[3,256,256]{2,1,0:T(8,128)(2,1)S(1)}, bf16[3,256,256]{2,1,0:T(8,128)(2,1)S(1)}) custom-call(s32[1,3]{1,0:T(1,128)S(1)} %bitcast.8, s32[64,64]{1,0:T(8,128)} %far_mask.1, bf16[3,256,256]{2,1,0:T(8,128)(2,1)} %bitcast.9), custom_call_target="tpu_custom_call" | custom-call | tf_op jit(solution)/shard_map/plan/pallas_call | solution.py:601
  5.0 0.0 copy-done.1
  5.0 0.0 copy-done.2
  5.0 30.0 %conditional.1 = (bf16[1,1,3,256,256]{4,3,2,1,0:T(8,128)(2,1)S(1)}) conditional(s32[]{:T(128)} %bitcast.7, (s32[8,128]{1,0:T(8,128)S(1)}, bf16[3,256,256]{2,1,0:T(8,128)(2,1)S(1)}, bf16[3,256,256]{2,1,0:T(8,128)(2,1)S(1)}) %tuple.25, (s32[8,128]{1,0:T(8,128)S(1)}, bf16[3,256,256]{2,1,0:T(8,128)(2,1)S(1)}, ...), branch_computations={%region_0.0_spmd, %region_1.0_spmd, %region_2.0_spmd, %region_3.0_... | conditional | bytes 8 | solution.py:866
  5.7 29.1 %sparse.4 = bf16[3,256,256]{2,1,0:T(8,128)(2,1)S(1)} custom-call(s32[8,128]{1,0:T(8,128)S(1)} %get-tuple-element.40.plan, bf16[3,256,256]{2,1,0:T(8,128)(2,1)S(1)} %get-tuple-element.42.canon, bf16[3,256,256]{2,1,0:T(8,128)(2,1)S(1)} %get-tuple-element.44.x_out), custom_call_target="tpu_custom_call" | custom-call | tf_op jit(solution)/shard_map/cond/branch_0_fun/sparse/pallas_call | solution.py:802
  35.0 0.7 %copy.15 = bf16[1,1,3,256,256]{4,3,2,1,0:T(8,128)(2,1)} copy(bf16[1,1,3,256,256]{4,3,2,1,0:T(8,128)(2,1)S(1)} %get-tuple-element.65) | data formatting | bytes 786432
Async XLA Ops:
  0.0 0.7 %copy-start = (s32[1,1,3]{2,1,0:T(1,128)S(1)}, s32[1,1,3]{2,1,0:T(1,128)}, u32[]{:S(2)}) copy-start(s32[1,1,3]{2,1,0:T(1,128)} %param.9) | copy-start | bytes 40
  0.0 5.0 %copy-start.1 = (bf16[1,1,3,256,256]{4,3,2,1,0:T(8,128)(2,1)S(1)}, bf16[1,1,3,256,256]{4,3,2,1,0:T(8,128)(2,1)}, u32[]{:S(2)}) copy-start(bf16[1,1,3,256,256]{4,3,2,1,0:T(8,128)(2,1)} %param.8) | copy-start | bytes 1179652
  0.7 4.4 %copy-start.2 = (s32[64,64]{1,0:T(8,128)S(1)}, s32[64,64]{1,0:T(8,128)}, u32[]{:S(2)}) copy-start(s32[64,64]{1,0:T(8,128)} %far_mask.1) | copy-start | bytes 49156
